TPU v7x, 32 devices: a 4x4x1 block of a 4x4x8 slice. The times are simulated.
32 devices in a mesh: rep: 1 (over z), r: 4 (over y), s: 8 (over x, core).
Axes of the slice: x: 4, y: 4, z: 1, core: 2. Of those that a mesh axis runs over, the one named last changes fastest.
The devices are a block of a 4x4x8 slice.
Arguments:
- x: bfloat16 [32, 2048, 1024], P(('rep', 'r', 's'))
- dy: bfloat16 [32, 2048, 1024], P(('rep', 'r', 's'))
- w_gate: bfloat16 [2, 1024, 3328], P(None, 's')
- w_up: bfloat16 [2, 1024, 3328], P(None, 's')
- w_down: bfloat16 [2, 3328, 1024], P(None, 's')
- m_w_gate: float32 [2, 1024, 3328], P(None, 's')
- m_w_up: float32 [2, 1024, 3328], P(None, 's')
- m_w_down: float32 [2, 3328, 1024], P(None, 's')
- v_w_gate: float32 [2, 1024, 3328], P(None, 's')
- v_w_up: float32 [2, 1024, 3328], P(None, 's')
- v_w_down: float32 [2, 3328, 1024], P(None, 's')
Outputs:
- output 1: bfloat16 [2, 1024, 3328], P('rep', 's')
- output 2: bfloat16 [2, 1024, 3328], P('rep', 's')
- output 3: bfloat16 [2, 3328, 1024], P('rep', 's')
- output 4: float32 [2, 1024, 3328], P('rep', 's')
- output 5: float32 [2, 1024, 3328], P('rep', 's')
- output 6: float32 [2, 3328, 1024], P('rep', 's')
- output 7: float32 [2, 1024, 3328], P('rep', 's')
- output 8: float32 [2, 1024, 3328], P('rep', 's')
- output 9: float32 [2, 3328, 1024], P('rep', 's')
All inputs are finite; a program needn't handle non-finite values.
Results may differ from a plain program's by a relative error of at most 0.022.
Values are sent between devices in bfloat16 or wider.
A program may use at most 768 MiB of HBM per device.

v0:
```python
import jax
import jax.numpy as jnp
from jax import lax
from jax.sharding import PartitionSpec as P

NAMES = ("w_gate", "w_up", "w_down")


def matmul(a, w):
    return jnp.dot(a, w, preferred_element_type=jnp.float32).astype(jnp.bfloat16)


def normed(h):
    wide = h.astype(jnp.float32)
    scale = lax.rsqrt(jnp.mean(wide**2, -1, keepdims=True) + 1e-6)
    return (wide * scale).astype(jnp.bfloat16)


def layer(h, w):
    a = normed(h)
    gate = jnp.dot(a, w["w_gate"], preferred_element_type=jnp.float32)
    up = jnp.dot(a, w["w_up"], preferred_element_type=jnp.float32)
    return h + matmul((jax.nn.silu(gate) * up).astype(jnp.bfloat16), w["w_down"])


def adamw(w, m, v, g):
    m = 0.9 * m + 0.1 * g
    v = 0.95 * v + 0.05 * g * g
    step = m * lax.rsqrt(v + 1e-8) + 0.1 * w
    return (w - 0.02 * step).astype(jnp.bfloat16), m, v


def solution(mesh):
    def fetched(weights, number):
        return {name: lax.all_gather(w[number], "s", axis=0, tiled=True) for name, w in zip(NAMES, weights, strict=True)}

    def summed(term):
        return lax.psum(lax.psum_scatter(term, "s", scatter_dimension=0, tiled=True), "r")

    def step(x, dy, *arrays):
        weights, m, v = (arrays[i : i + 3] for i in (0, 3, 6))
        layers = weights[0].shape[0]
        h, kept = x[0], []
        for number in range(layers):
            kept.append(h)
            h = layer(h, fetched(weights, number))
        by_h, mine = dy[0], [None] * layers
        for number in reversed(range(layers)):
            _, back = jax.vjp(lambda w, h: layer(h, w), fetched(weights, number), kept[number])
            by_w, by_h = back(by_h)
            mine[number] = [summed(by_w[name]) for name in NAMES]
        gradients = [jnp.stack([mine[number][i] for number in range(layers)]).astype(jnp.float32) for i in range(3)]
        new = [adamw(w.astype(jnp.float32), m, v, g) for w, m, v, g in zip(weights, m, v, gradients, strict=True)]
        return tuple(one[which] for which in range(3) for one in new)

    states, cut = P(("rep", "r", "s"), None, None), P(None, "s", None)
    return jax.shard_map(
        step,
        mesh=mesh,
        in_specs=(states, states) + (cut,) * 9,
        out_specs=(P("rep", "s", None),) * 9,
        check_vma=False,
    )
```

profile of v0, /device:TPU:97, one launch (start us, length us, event | category | flops | bytes accessed | tf_op | source)
XLA Modules:
  0.0 775.6 jit_solution(1702564215105138096)
XLA Ops:
  7.3 2.8 fusion.88
  16.4 6.5 copy.20
  23.0 3.1 fusion.15
  26.1 6.5 copy.21
  32.6 22.3 %all-gather.13.cloned.1.call-done = bf16[1,1024,3328]{2,1,0:T(8,128)(2,1)} async-done(((bf16[1,128,3328]{2,1,0:T(8,128)(2,1)}), bf16[1,1024,3328]{2,1,0:T(8,128)(2,1)}) %all-gather.13.cloned.1.call-update) | async-done | bytes 6815760 | tf_op jit(solution)/shard_map/all_gather | solution.py:35
  54.9 23.2 %fusion.41 = f32[2048,3328]{1,0:T(8,128)} fusion(bf16[1,1024,3328]{2,1,0:T(8,128)(2,1)} %all-gather.13.cloned.1.call-done, bf16[1,2048,1024]{1,2,0:T(8,128)(2,1)} %copy.20, f32[2048]{0:T(1024)S(1)} %add_rsqrt_fusion), kind=kOutput, calls=%fused_computation.59 | convolution fusion | flops 13964935168 | bytes 38281216 | tf_op jit(solution)/shard_map/dot_general | solution.py:21
  78.1 19.5 %all-gather.15.cloned.1.call-done = bf16[1,1024,3328]{2,1,0:T(8,128)(2,1)} async-done(((bf16[1,128,3328]{2,1,0:T(8,128)(2,1)}), bf16[1,1024,3328]{2,1,0:T(8,128)(2,1)}) %all-gather.15.cloned.1.call-update) | async-done | bytes 6815760 | tf_op jit(solution)/shard_map/all_gather | solution.py:35
  97.5 32.1 %multiply_convert_fusion.1 = (bf16[2048,3328]{1,0:T(8,128)(2,1)}, f32[2048,3328]{1,0:T(8,128)}) fusion(f32[2048,3328]{1,0:T(8,128)} %fusion.41, bf16[1,1024,3328]{2,1,0:T(8,128)(2,1)} %all-gather.15.cloned.1.call-done, bf16[1,2048,1024]{1,2,0:T(8,128)(2,1)} %copy.20, f32[2048]{0:T(1024)S(1)} %add_rsqrt_fusion), kind=kOutput, calls=%fused_computation.17 | convolution fusion | flops 14005829632 | bytes 79175680 | tf_op jit(solution)/shard_map/dot_general | solution.py:22
  129.7 10.5 %all-gather.17.cloned.1.call-done = bf16[1,3328,1024]{2,1,0:T(8,128)(2,1)} async-done(((bf16[1,416,1024]{2,1,0:T(8,128)(2,1)}), bf16[1,3328,1024]{2,1,0:T(8,128)(2,1)}) %all-gather.17.cloned.1.call-update) | async-done | bytes 6815760 | tf_op jit(solution)/shard_map/all_gather | solution.py:35
  140.2 22.2 %fusion.19 = (f32[2048]{0:T(1024)S(1)}, bf16[2048,1024]{0,1:T(8,128)(2,1)}) fusion(bf16[2048,3328]{1,0:T(8,128)(2,1)} %get-tuple-element.30, bf16[1,3328,1024]{2,1,0:T(8,128)(2,1)} %all-gather.17.cloned.1.call-done, bf16[1,2048,1024]{1,2,0:T(8,128)(2,1)} %copy.20), kind=kOutput, calls=%fused_computation.37 | convolution fusion | flops 13969127424 | bytes 28844032 | tf_op jit(solution)/shard_map/dot_general | solution.py:10
  162.3 20.3 %all-gather.23.cloned.1.call-done = bf16[1,1024,3328]{2,1,0:T(8,128)(2,1)} async-done(((bf16[1,128,3328]{2,1,0:T(8,128)(2,1)}), bf16[1,1024,3328]{2,1,0:T(8,128)(2,1)}) %all-gather.23.cloned.1.call-update) | async-done | bytes 6815760 | tf_op jit(solution)/shard_map/all_gather | solution.py:35
  182.7 23.5 %fusion.28 = f32[2048,3328]{1,0:T(8,128)} fusion(bf16[1,1024,3328]{2,1,0:T(8,128)(2,1)} %all-gather.23.cloned.1.call-done, bf16[2048,1024]{0,1:T(8,128)(2,1)} %get-tuple-element.33, f32[2048]{0:T(1024)S(1)} %fusion.74), kind=kOutput, calls=%fused_computation.46 | convolution fusion | flops 13964935168 | bytes 38281216 | tf_op jit(solution)/shard_map/jvp()/dot_general | solution.py:22
  206.2 19.0 %all-gather.21.cloned.1.call-done = bf16[1,3328,1024]{2,1,0:T(8,128)(2,1)} async-done(((bf16[1,416,1024]{2,1,0:T(8,128)(2,1)}), bf16[1,3328,1024]{2,1,0:T(8,128)(2,1)}) %all-gather.21.cloned.1.call-update) | async-done | bytes 6815760 | tf_op jit(solution)/shard_map/all_gather | solution.py:35
  225.2 21.0 %convolution_convert_fusion.1 = bf16[2048,3328]{1,0:T(8,128)(2,1)} fusion(bf16[1,3328,1024]{2,1,0:T(8,128)(2,1)} %all-gather.21.cloned.1.call-done, bf16[1,2048,1024]{2,1,0:T(8,128)(2,1)} %param.12), kind=kOutput, calls=%fused_computation.23 | convolution fusion | flops 13965459456 | bytes 24641536 | tf_op jit(solution)/shard_map/transpose(jvp())/dot_general | solution.py:10
  246.2 21.5 %all-gather.19.cloned.1.call-done = bf16[1,1024,3328]{2,1,0:T(8,128)(2,1)} async-done(((bf16[1,128,3328]{2,1,0:T(8,128)(2,1)}), bf16[1,1024,3328]{2,1,0:T(8,128)(2,1)}) %all-gather.19.cloned.1.call-update) | async-done | bytes 6815760 | tf_op jit(solution)/shard_map/all_gather | solution.py:35
  267.7 39.6 %fusion.2 = (bf16[2048,3328]{1,0:T(8,128)(2,1)}, f32[2048,3328]{1,0:T(8,128)}) fusion(f32[2048,3328]{1,0:T(8,128)} %fusion.28, bf16[2048,3328]{1,0:T(8,128)(2,1)} %convolution_convert_fusion.1, bf16[1,1024,3328]{2,1,0:T(8,128)(2,1)} %all-gather.19.cloned.1.call-done, bf16[2048,1024]{0,1:T(8,128)(2,1)} %get-tuple-element.33, f32[2048]{0:T(1024)S(1)} %fusion.74), kind=kOutput, calls=%fused_computation.8 | convolution fusion | flops 14046724096 | bytes 92807168 | tf_op jit(solution)/shard_map/jvp()/dot_general | solution.py:21
  307.2 23.1 %fusion.12 = bf16[2048,1024]{0,1:T(8,128)(2,1)} fusion(bf16[2048,3328]{1,0:T(8,128)(2,1)} %convolution_convert_fusion.1, bf16[1,1024,3328]{2,1,0:T(8,128)(2,1)} %all-gather.23.cloned.1.call-done, f32[2048,3328]{1,0:T(8,128)} %get-tuple-element.35), kind=kOutput, calls=%fused_computation.21 | convolution fusion | flops 13999538176 | bytes 51904512 | tf_op jit(solution)/shard_map/transpose(jvp())/dot_general | solution.py:22
  330.4 21.7 %fusion.21 = (f32[2048]{0:T(1024)S(1)}, bf16[2048,1024]{0,1:T(8,128)(2,1)}) fusion(bf16[2048,1024]{0,1:T(8,128)(2,1)S(1)} %copy-done.5, bf16[2048,1024]{0,1:T(8,128)(2,1)} %fusion.12, bf16[2048,3328]{1,0:T(8,128)(2,1)} %get-tuple-element.34, bf16[1,1024,3328]{2,1,0:T(8,128)(2,1)} %all-gather.19.cloned.1.call-done), kind=kOutput, calls=%fused_computation.39 | convolution fusion | flops 13969127424 | bytes 33038336 | tf_op jit(solution)/shard_map/transpose(jvp())/dot_general | solution.py:21
  352.1 4.9 fusion.44
  359.0 19.6 %convolution_convert_fusion.2 = bf16[3328,1024]{1,0:T(8,128)(2,1)} fusion(bf16[2048,3328]{1,0:T(8,128)(2,1)} %get-tuple-element.30, bf16[2048,1024]{0,1:T(8,128)(2,1)S(1)} %fusion.44), kind=kOutput, calls=%fused_computation.44 | convolution fusion | flops 13962051584 | bytes 24641536 | tf_op jit(solution)/shard_map/transpose(jvp())/dot_general | solution.py:10
  378.7 27.6 %fusion.25 = bf16[3328,1024]{1,0:T(8,128)(2,1)} fusion(f32[2048,3328]{1,0:T(8,128)} %fusion.28, bf16[1,2048,1024]{2,1,0:T(8,128)(2,1)} %param.12, f32[2048,3328]{1,0:T(8,128)} %get-tuple-element.35), kind=kOutput, calls=%fused_computation.41 | convolution fusion | flops 14002946048 | bytes 65536000 | tf_op jit(solution)/shard_map/transpose(jvp())/dot_general | solution.py:10
  406.5 21.1 %convolution_convert_fusion = bf16[2048,3328]{1,0:T(8,128)(2,1)} fusion(bf16[2048,1024]{0,1:T(8,128)(2,1)} %copy-done.6, bf16[1,3328,1024]{2,1,0:T(8,128)(2,1)} %all-gather.17.cloned.1.call-done), kind=kOutput, calls=%fused_computation.22 | convolution fusion | flops 13965459456 | bytes 24641536 | tf_op jit(solution)/shard_map/transpose(jvp())/dot_general | solution.py:10
  427.6 25.5 %fusion.27 = bf16[1024,3328]{1,0:T(8,128)(2,1)} fusion(bf16[2048,3328]{1,0:T(8,128)(2,1)} %convolution_convert_fusion, f32[2048,3328]{1,0:T(8,128)} %fusion.41, bf16[1,2048,1024]{1,2,0:T(8,128)(2,1)} %copy.20, f32[2048]{0:T(1024)S(1)} %copy-done.19), kind=kOutput, calls=%fused_computation.43 | convolution fusion | flops 14009237504 | bytes 51912704 | tf_op jit(solution)/shard_map/transpose(jvp())/dot_general | solution.py:22
  453.8 25.4 %fusion.26 = bf16[1024,3328]{1,0:T(8,128)(2,1)} fusion(bf16[2048,3328]{1,0:T(8,128)(2,1)} %convolution_convert_fusion.1, bf16[2048,1024]{0,1:T(8,128)(2,1)} %get-tuple-element.33, f32[2048]{0:T(1024)S(1)} %copy-done.15, f32[2048,3328]{1,0:T(8,128)} %get-tuple-element.35), kind=kOutput, calls=%fused_computation.42 | convolution fusion | flops 14009237504 | bytes 51912704 | tf_op jit(solution)/shard_map/transpose(jvp())/dot_general | solution.py:22
  479.3 31.2 %fusion.22 = bf16[1024,3328]{1,0:T(8,128)(2,1)} fusion(f32[2048,3328]{1,0:T(8,128)} %fusion.41, f32[2048,3328]{1,0:T(8,128)} %get-tuple-element.31, bf16[2048,3328]{1,0:T(8,128)(2,1)} %convolution_convert_fusion, bf16[1,2048,1024]{1,2,0:T(8,128)(2,1)} %copy.20, f32[2048]{0:T(1024)S(1)} %copy-done.19), kind=kOutput, calls=%fused_computation.40 | convolution fusion | flops 14043316224 | bytes 79175680 | tf_op jit(solution)/shard_map/transpose(jvp())/dot_general | solution.py:21
  510.6 21.3 %convolution_convert_fusion.3 = bf16[1024,3328]{1,0:T(8,128)(2,1)} fusion(bf16[2048,3328]{1,0:T(8,128)(2,1)} %get-tuple-element.34, bf16[2048,1024]{0,1:T(8,128)(2,1)} %get-tuple-element.33, f32[2048]{0:T(1024)S(1)} %copy-done.15), kind=kOutput, calls=%fused_computation.45 | convolution fusion | flops 13964935168 | bytes 24649728 | tf_op jit(solution)/shard_map/transpose(jvp())/dot_general | solution.py:21
  532.1 21.9 %reduce-scatter.13.cloned.1.call-done = bf16[128,3328]{1,0:T(8,128)(2,1)} async-done(((bf16[1024,3328]{1,0:T(8,128)(2,1)}), bf16[128,3328]{1,0:T(8,128)(2,1)}) %reduce-scatter.13.cloned.1.call-update) | async-done | bytes 851984 | tf_op jit(solution)/shard_map/reduce_scatter | solution.py:38
  554.0 44.5 %reduce-scatter.7.cloned.1.call-done = bf16[128,3328]{1,0:T(8,128)(2,1)} async-done(((bf16[1024,3328]{1,0:T(8,128)(2,1)}), bf16[128,3328]{1,0:T(8,128)(2,1)}) %reduce-scatter.7.cloned.1.call-update) | async-done | bytes 851984 | tf_op jit(solution)/shard_map/reduce_scatter | solution.py:38
  598.5 44.4 %reduce-scatter.9.cloned.1.call-done = bf16[128,3328]{1,0:T(8,128)(2,1)} async-done(((bf16[1024,3328]{1,0:T(8,128)(2,1)}), bf16[128,3328]{1,0:T(8,128)(2,1)}) %reduce-scatter.9.cloned.1.call-update) | async-done | bytes 851984 | tf_op jit(solution)/shard_map/reduce_scatter | solution.py:38
  642.9 105.2 %all-reduce.3.cloned.1.call-done = (bf16[1,128,3328]{2,1,0:T(8,128)(2,1)}, bf16[1,128,3328]{2,1,0:T(8,128)(2,1)}, bf16[1,128,3328]{2,1,0:T(8,128)(2,1)}, bf16[1,...) async-done(((bf16[1,128,3328]{2,1,0:T(8,128)(2,1)}, bf16[1,128,3328]{2,1,0:T(8,128)(2,1)}, bf16[1,128,3328]{2,1,0:T(8,128)(2,1)}, ...) | async-done | bytes 5111824 | tf_op jit(solution)/shard_map/psum | solution.py:38
  748.2 7.6 fusion.61
  759.4 9.2 %fusion.53 = (bf16[2,128,3328]{2,1,0:T(8,128)(2,1)}, f32[2,128,3328]{2,1,0:T(8,128)}, f32[2,128,3328]{2,1,0:T(8,128)}, bf16[2,128,3328]{2,1,0:T(8,128)(2,1)}, f3...) fusion(bf16[2,128,3328]{2,1,0:T(8,128)(2,1)S(1)} %copy-done.3, bf16[1,128,3328]{2,1,0:T(8,128)(2,1)S(1)} %copy-done.10, ...), kind=kLoop, calls=%fused_computation.80 | loop fusion | flops 32374784 | bytes 37486592 | tf_op jit(solution)/shard_map/convert_element_type | solution.py:30
  (74 shorter events, 13.4 us)
Async XLA Ops:
  7.2 5.9 copy-start.1
  7.2 47.7 %all-gather.13.cloned.1.call-start = ((), (), s32[]{:S(2)}) async-start(), calls=%async_computation.12 | async-start | bytes 7667712 | tf_op jit(solution)/shard_map/all_gather | solution.py:35
  10.1 87.4 %all-gather.15.cloned.1.call-start = ((), (), s32[]{:S(2)}) async-start(), calls=%async_computation.13 | async-start | bytes 7667712 | tf_op jit(solution)/shard_map/all_gather | solution.py:35
  13.0 127.2 %all-gather.17.cloned.1.call-start = ((), (), s32[]{:S(2)}) async-start(), calls=%async_computation.14 | async-start | bytes 7667712 | tf_op jit(solution)/shard_map/all_gather | solution.py:35
  14.4 168.2 %all-gather.23.cloned.1.call-start = ((), (), s32[]{:S(2)}) async-start(), calls=%async_computation.17 | async-start | bytes 7667712 | tf_op jit(solution)/shard_map/all_gather | solution.py:35
  15.1 210.1 %all-gather.21.cloned.1.call-start = ((), (), s32[]{:S(2)}) async-start(), calls=%async_computation.16 | async-start | bytes 7667712 | tf_op jit(solution)/shard_map/all_gather | solution.py:35
  15.7 251.9 %all-gather.19.cloned.1.call-start = ((), (), s32[]{:S(2)}) async-start(), calls=%async_computation.15 | async-start | bytes 7667712 | tf_op jit(solution)/shard_map/all_gather | solution.py:35
  16.4 515.7 %reduce-scatter.15.cloned.1.call-start = ((), (), s32[]{:S(2)}) async-start(), calls=%async_computation.10 | async-start | bytes 7667712 | tf_op jit(solution)/shard_map/reduce_scatter | solution.py:38
  26.0 71.5 %copy-start.18 = (f32[2048]{0:T(1024)}, f32[2048]{0:T(1024)S(1)}, u32[]{:S(2)}) copy-start(f32[2048]{0:T(1024)S(1)} %add_rsqrt_fusion) | copy-start | bytes 24580
  162.3 43.9 %copy-start.16 = (f32[2048]{0:T(1024)}, f32[2048]{0:T(1024)S(1)}, u32[]{:S(2)}) copy-start(f32[2048]{0:T(1024)S(1)} %get-tuple-element.32) | copy-start | bytes 24580
  162.3 189.8 %copy-start.14 = (f32[2048]{0:T(1024)}, f32[2048]{0:T(1024)S(1)}, u32[]{:S(2)}) copy-start(f32[2048]{0:T(1024)S(1)} %fusion.74) | copy-start | bytes 24580
  307.2 23.1 %copy-start.5 = (bf16[2048,1024]{0,1:T(8,128)(2,1)S(1)}, bf16[2048,1024]{0,1:T(8,128)(2,1)}, u32[]{:S(2)}) copy-start(bf16[2048,1024]{0,1:T(8,128)(2,1)} %get-tuple-element.33) | copy-start | bytes 12582916
  330.4 21.7 %copy-start.17 = (f32[2048]{0:T(1024)S(1)}, f32[2048]{0:T(1024)}, u32[]{:S(2)}) copy-start(f32[2048]{0:T(1024)} %copy-done.16) | copy-start | bytes 24580
  330.4 21.7 %copy-start = (bf16[1,2048,1024]{1,2,0:T(8,128)(2,1)S(1)}, bf16[1,2048,1024]{1,2,0:T(8,128)(2,1)}, u32[]{:S(2)}) copy-start(bf16[1,2048,1024]{1,2,0:T(8,128)(2,1)} %copy.21) | copy-start | bytes 12582916
  357.0 2.0 copy-start.6
  378.7 153.4 %reduce-scatter.17.cloned.1.call-start = ((), (), s32[]{:S(2)}) async-start(), calls=%async_computation.11 | async-start | bytes 7667712 | tf_op jit(solution)/shard_map/reduce_scatter | solution.py:38
  406.4 21.2 %copy-start.19 = (f32[2048]{0:T(1024)S(1)}, f32[2048]{0:T(1024)}, u32[]{:S(2)}) copy-start(f32[2048]{0:T(1024)} %copy-done.18) | copy-start | bytes 24580
  406.4 125.7 %reduce-scatter.11.cloned.1.call-start = ((), (), s32[]{:S(2)}) async-start(), calls=%async_computation.8 | async-start | bytes 7667712 | tf_op jit(solution)/shard_map/reduce_scatter | solution.py:38
  453.2 100.8 %reduce-scatter.13.cloned.1.call-start = ((), (), s32[]{:S(2)}) async-start(), calls=%async_computation.9 | async-start | bytes 7667712 | tf_op jit(solution)/shard_map/reduce_scatter | solution.py:38
  479.2 119.3 %reduce-scatter.7.cloned.1.call-start = ((), (), s32[]{:S(2)}) async-start(), calls=%async_computation.6 | async-start | bytes 7667712 | tf_op jit(solution)/shard_map/reduce_scatter | solution.py:38
  510.5 132.3 %reduce-scatter.9.cloned.1.call-start = ((), (), s32[]{:S(2)}) async-start(), calls=%async_computation.7 | async-start | bytes 7667712 | tf_op jit(solution)/shard_map/reduce_scatter | solution.py:38
  531.9 216.2 %copy-start.2 = (bf16[2,416,1024]{2,1,0:T(8,128)(2,1)S(1)}, bf16[2,416,1024]{2,1,0:T(8,128)(2,1)}, u32[]{:S(2)}) copy-start(bf16[2,416,1024]{2,1,0:T(8,128)(2,1)} %param.15) | copy-start | bytes 5111812
  532.0 216.2 %all-reduce.3.cloned.1.call-start = ((), (), s32[]{:S(2)}) async-start(), calls=%async_computation.18 | async-start | bytes 10223616 | tf_op jit(solution)/shard_map/psum | solution.py:38
  748.1 7.6 copy-start.3
  748.1 7.6 copy-start.4
  748.1 8.0 %copy-start.7 = (f32[2,128,3328]{2,1,0:T(8,128)S(1)}, f32[2,128,3328]{2,1,0:T(8,128)}, u32[]{:S(2)}) copy-start(f32[2,128,3328]{2,1,0:T(8,128)} %param.19) | copy-start | bytes 10223620
  748.1 9.4 %copy-start.8 = (f32[2,128,3328]{2,1,0:T(8,128)S(1)}, f32[2,128,3328]{2,1,0:T(8,128)}, u32[]{:S(2)}) copy-start(f32[2,128,3328]{2,1,0:T(8,128)} %param.16) | copy-start | bytes 10223620
  748.2 10.4 %copy-start.9 = (f32[2,128,3328]{2,1,0:T(8,128)S(1)}, f32[2,128,3328]{2,1,0:T(8,128)}, u32[]{:S(2)}) copy-start(f32[2,128,3328]{2,1,0:T(8,128)} %param.20) | copy-start | bytes 10223620
  748.2 10.5 %copy-start.10 = (bf16[1,128,3328]{2,1,0:T(8,128)(2,1)S(1)}, bf16[1,128,3328]{2,1,0:T(8,128)(2,1)}, u32[]{:S(2)}) copy-start(bf16[1,128,3328]{2,1,0:T(8,128)(2,1)} %get-tuple-element.9) | copy-start | bytes 2555908
  748.2 10.7 %copy-start.11 = (bf16[1,128,3328]{2,1,0:T(8,128)(2,1)S(1)}, bf16[1,128,3328]{2,1,0:T(8,128)(2,1)}, u32[]{:S(2)}) copy-start(bf16[1,128,3328]{2,1,0:T(8,128)(2,1)} %get-tuple-element.10) | copy-start | bytes 2555908
  748.2 11.0 %copy-start.12 = (bf16[1,128,3328]{2,1,0:T(8,128)(2,1)S(1)}, bf16[1,128,3328]{2,1,0:T(8,128)(2,1)}, u32[]{:S(2)}) copy-start(bf16[1,128,3328]{2,1,0:T(8,128)(2,1)} %get-tuple-element.11) | copy-start | bytes 2555908
  748.2 11.2 %copy-start.13 = (bf16[1,128,3328]{2,1,0:T(8,128)(2,1)S(1)}, bf16[1,128,3328]{2,1,0:T(8,128)(2,1)}, u32[]{:S(2)}) copy-start(bf16[1,128,3328]{2,1,0:T(8,128)(2,1)} %get-tuple-element.12) | copy-start | bytes 2555908
  (1 other events, 0.7 us)
Sparse Core Ops, SparseCore 0:
  10.3 44.5 all-gather.12
  57.1 40.4 all-gather.14
  99.7 40.4 all-gather.16
  142.2 40.4 all-gather.22
  184.7 40.4 all-gather.20
  227.2 40.4 all-gather.18
  378.8 41.7 reduce-scatter.14
  422.9 42.1 reduce-scatter.16
  467.4 42.1 reduce-scatter.10
  511.8 42.1 reduce-scatter.12
  556.3 42.1 reduce-scatter.6
  600.7 42.1 reduce-scatter.8
  645.7 102.4 all-reduce.2
where the time goes:
time: 783 us; the launch traced here: 776 us
  matrix products  378 us (48%)
  waiting for transfers between devices  331 us (42%)
  local copies, waits for them, and re-layouts  26.1 us (3%)
  other arithmetic  24.8 us (3%)
  between operations  14.6 us (2%)
    dot_general x5, matrix products, layer(): gate = jnp.dot(a, w['w_gate'], preferred_element_type=jnp.float32)  137 us
    dot_general x5, matrix products, layer(): up = jnp.dot(a, w['w_up'], preferred_element_type=jnp.float32)  130 us
    all_gather x6, waiting for transfers between devices, fetched(): lax.all_gather(w[number], 's', axis=0, tiled=True)  113 us
    dot_general x5, matrix products, matmul(): jnp.dot(a, w, preferred_element_type=jnp.float32).astype(jnp.bfloat16)  111 us
    reduce_scatter x6, waiting for transfers between devices, summed(): lax.psum_scatter(term, 's', scatter_dimension=0, tiled=True)  111 us
    psum x1, waiting for transfers between devices, summed(): lax.psum(lax.psum_scatter(term, 's', scatter_dimension=0, tiled=True), 'r')  105 us
    unnamed x42, local copies, waits for them, and re-layouts  19.3 us
    convert_element_type x2, other arithmetic, adamw(): return ((w - 0.02 * step).astype(jnp.bfloat16), m, v)  16.8 us
  transfers between devices with their start and end apart: 13, of which 10 were waited for; matrix products, arithmetic and copies ran while one was open for 38% of the time, Pallas kernels for 0%

commit v1 on v0

v1 whole, which is shorter than its diff:
```python
import functools
import jax
import jax.numpy as jnp
from jax import lax
from jax.experimental import pallas as pl
from jax.experimental.pallas import tpu as pltpu
from jax.sharding import PartitionSpec as P

bf16, f32 = jnp.bfloat16, jnp.float32
C = 256
W = C + C
R = 256
MESH = pl.DeviceIdType.MESH
NN, NT = ((1,), (0,)), ((1,), (1,))


def dot(a, b, dims):
    return lax.dot_general(a, b, (dims, ((), ())), preferred_element_type=f32)


def ds(i, n):
    return pl.ds(pl.multiple_of(i * n, n), n)


def loop(first, last, f):
    def body(i, _):
        f(i)
        return 0
    lax.fori_loop(first, last, body, 0)


def place():
    z, y, s = (lax.axis_index(n) for n in ("rep", "r", "s"))
    x, c = s // 2, s % 2

    def pair(i):
        near, far = i + 1 - 2 * (i % 2), 3 - i
        return (1 - c) * near + c * far, c * near + (1 - c) * far

    return z, y, x, c, pair(x), pair(y)


def barrier(z, y, x, c, xs):
    sem = pltpu.get_barrier_semaphore()
    others = [(z, y, 2 * x + 1 - c)] + [(z, y, 2 * p + c) for p in xs] + [(z, (y + d) % 4, 2 * x + c) for d in (1, 3)]
    for o in others:
        pl.semaphore_signal(sem, inc=1, device_id=o, device_id_type=MESH)
    pl.semaphore_wait(sem, len(others))


class Gather:
    def __init__(self, where, own, full, block, width, sems):
        self.z, self.y, self.x, self.c, (self.p1, self.p2), _ = where
        self.own, self.full, self.block, self.width = own, full, block, width
        self.a, self.b1, self.b2, self.ys, self.e, self.s = sems
        self.opp = (self.x + 2) % 4
        self.o = 1 - self.c
        self.par = self.y % 2

    def dev(self, x=None, y=None, c=None):
        x, y, c = (self.x if x is None else x), (self.y if y is None else y), (self.c if c is None else c)
        return (self.z, y, 2 * x + c)

    def part(self, x, off, n, k, c=None):
        c = self.c if c is None else c
        row = pl.multiple_of((2 * x + c) * self.block + off, self.block // 4)
        return self.full.at[k, pl.ds(row, n), :]

    def mine(self, off, n, k):
        if self.own is None:
            return self.part(self.x, off, n, k)
        return self.own.at[pl.ds(pl.multiple_of(off, self.block // 4), n), ds(k, self.width)]

    def send(self, src, dst, sem, k, to):
        return pltpu.make_async_remote_copy(src, dst, self.s.at[k], sem.at[k], device_id=to, device_id_type=MESH)

    def first(self, k):
        h = self.block // 2
        o = self.par * h
        return [
            self.send(self.mine(o, h, k), self.part(self.x, o, h, k), self.a, k, self.dev(x=self.p1)),
            self.send(self.mine(o, h, k), self.part(self.x, o, h, k), self.b1, k, self.dev(x=self.p2)),
            self.send(self.mine(0, self.block, k), self.part(self.x, 0, self.block, k), self.e, k, self.dev(c=self.o)),
        ]

    def across(self, x, k):
        q = self.block // 4
        o = self.par * 2 * q
        return [
            self.send(self.part(x, o, q, k), self.part(x, o, q, k), self.ys, k, self.dev(y=(self.y + 1) % 4)),
            self.send(self.part(x, o + q, q, k), self.part(x, o + q, q, k), self.ys, k, self.dev(y=(self.y + 3) % 4)),
        ]

    def over(self, x, half, k):
        h = self.block // 2
        return [self.send(self.part(x, half * h, h, k), self.part(x, half * h, h, k), self.e, k, self.dev(c=self.o))]

    def second(self, k):
        h = self.block // 2
        o = self.par * h
        fwd = [self.send(self.part(self.p1, o, h, k), self.part(self.p1, o, h, k), self.b2, k, self.dev(x=self.p2))]
        return fwd + self.across(self.p1, k) + self.across(self.p2, k) + self.over(self.p1, self.par, k) + self.over(self.p2, self.par, k)

    def third(self, k):
        return self.across(self.opp, k) + self.over(self.opp, self.par, k)

    def fourth(self, k):
        return [d for x in (self.p1, self.p2, self.opp) for d in self.over(x, 1 - self.par, k)]

    def got(self, sem, rows, k):
        r = self.full.at[0, pl.ds(0, rows), :]
        pltpu.make_async_copy(r, r, sem.at[k]).wait()

    def stage(self, i, k):
        h, q = self.block // 2, self.block // 4
        if i == 0:
            sent = self.first(k)
        elif i == 1:
            self.got(self.a, h, k)
            self.got(self.b1, h, k)
            sent = self.second(k)
        elif i == 2:
            self.got(self.b2, h, k)
            sent = self.third(k)
        elif i == 3:
            self.got(self.ys, 6 * q, k)
            sent = self.fourth(k)
        else:
            self.got(self.e, 4 * self.block, k)
            self.got(self.s, 7 * self.block, k)
            return
        for d in sent:
            d.start()


LAGS = (0, 2, 4, 6, 8)


def norm(h):
    wide = h.astype(f32)
    return (wide * lax.rsqrt(jnp.mean(wide * wide, -1, keepdims=True) + 1e-6)).astype(bf16)


dma = pltpu.SemaphoreType.DMA


def turned(to, r, v, size, c):
    t = v.T
    chips = to.shape[0] // size // 2
    for b in range(2 * chips):
        to[ds(chips * ((b + c) % 2) + b // 2, size), r] = t[b * size : (b + 1) * size]


def own_load(w_g, w_u, l, own, sem):
    def one(k):
        for j, w in ((0, w_g), (1, w_u)):
            pltpu.make_async_copy(w.at[l, :, ds(k, C)], own.at[:, ds(2 * k + j, C)], sem).start()
    loop(0, own.shape[1] // (W), one)


def forward_kernel(tm, early, x_h, wg_h, wu_h, wd_h, fgu0, fgu1, fd0, fd1, a0t_h, h1_h, a1_h, a1t_h, act_h, ab_h,
                   xv, av, tv, actv, abv, wv, wdv, own0, own1, ownd, isem, wsem, absem, actsem, own_sem, *gs):
    T, D = x_h.shape
    F = fd0.shape[1]
    n = F // C
    nd = D // C
    where = place()
    z, y, x, c, xs, ys = where
    s = 2 * x + c
    own_load(wg_h, wu_h, 0, own0, own_sem.at[0])
    own_load(wg_h, wu_h, 1, own1, own_sem.at[1])
    xin = pltpu.make_async_copy(x_h, xv, isem.at[0])
    xin.start()
    din = pltpu.make_async_copy(wd_h, ownd, isem.at[1])
    din.start()
    barrier(z, y, x, c, xs)
    for l, own in ((0, own0), (1, own1)):
        pltpu.make_async_copy(own, own, own_sem.at[l]).wait()
    rows, drows = own0.shape[0], wd_h.shape[1]
    kept = ((own0, fgu0), (own1, fgu1), (ownd.at[0], fd0), (ownd.at[1], fd1))

    def keep(i, k):
        own, full = kept[i]
        return pltpu.make_async_copy(own.at[:, ds(k, full.shape[2])], full.at[k, ds(s, own.shape[0]), :], own_sem.at[i])

    g0 = Gather(where, own0, fgu0, rows, W, gs[:6])
    d0 = Gather(where, wd_h.at[0], fd0, drows, C, gs[6:12])
    d1 = Gather(where, wd_h.at[1], fd1, drows, C, gs[12:18])
    g1 = Gather(where, own1, fgu1, rows, W, gs[18:])
    units = ((g0, 0, n), (d0, n, nd), (d1, n + nd, nd), (g1, n + 2 * nd, early))
    total = n + 2 * nd + early

    def tick(t):
        for i, lag in enumerate(LAGS):
            u = t - lag
            for g, base, count in units:
                @pl.when((u >= base) & (u < base + count))
                def _(g=g, i=i, k=u - base):
                    g.stage(i, k)

    lead = LAGS[-1]
    for t in range(2):
        tick(t)
    din.wait()
    for i, (own, full) in enumerate(kept):
        loop(0, full.shape[0], lambda k, i=i: keep(i, k).start())
    xin.wait()

    def start(i):
        r = ds(i, R)
        a = norm(xv[r, :])
        av[r, :] = a
        turned(tv, r, a, rows, c)
    loop(0, T // R, start)
    out0 = pltpu.make_async_copy(tv, a0t_h, isem.at[0])
    out0.start()
    loop(2, lead, lambda t: tick(t))
    for i, (own, full) in enumerate(kept):
        pltpu.make_async_copy(own, own, own_sem.at[i]).wait()

    def wload(k, slot):
        return pltpu.make_async_copy(fgu0.at[k], wv.at[slot], wsem.at[slot])

    def abstore(k, slot):
        return pltpu.make_async_copy(abv.at[slot], ab_h.at[k], absem.at[slot])

    tick(lead)
    wload(0, 0).start()

    def up(k):
        slot = k % 2
        tick(k + 1 + lead)

        @pl.when(k + 1 < n)
        def _():
            wload(k + 1, 1 - slot).start()
        wload(k, slot).wait()

        @pl.when(k >= 2)
        def _():
            abstore(k - 2, slot).wait()

        for i in range(T // tm):
            r = pl.ds(i * tm, tm)
            gu = dot(av[r, :], wv[slot], NN)
            g, u = gu[:, :C], gu[:, C:]
            sg = 0.5 + 0.5 * jnp.tanh(0.5 * g)
            b = g * sg
            actv[r, ds(k, C)] = (b * u).astype(bf16)
            abv[slot, r, :C] = u * (sg + b * (1 - sg))
            abv[slot, r, C:] = b
        abstore(k, slot).start()
        pltpu.make_async_copy(actv.at[:, ds(k, C)], act_h.at[k], actsem).start()
    loop(0, n, up)

    def dload(j, slot):
        return pltpu.make_async_copy(fd0.at[j], wdv.at[slot], wsem.at[2 + slot])

    dload(0, 0).start()
    out0.wait()

    def down(j):
        slot = j % 2
        tick(n + j + 1 + lead)

        @pl.when(j + 1 < nd)
        def _():
            dload(j + 1, 1 - slot).start()
        dload(j, slot).wait()
        for i in range(T // tm):
            r = pl.ds(i * tm, tm)
            av[r, ds(j, C)] = dot(actv[r, :], wdv[slot], NN).astype(bf16)
    loop(0, nd, down)
    for k in (n - 2, n - 1):
        abstore(k, k % 2).wait()
    pltpu.make_async_copy(act_h, act_h, actsem).wait()

    def mid(i):
        r = ds(i, R)
        h = (xv[r, :].astype(f32) + av[r, :].astype(f32)).astype(bf16)
        xv[r, :] = h
        a = norm(h)
        av[r, :] = a
        turned(tv, r, a, rows, c)
    loop(0, T // R, mid)
    outs = [pltpu.make_async_copy(v, h, isem.at[i]) for i, (v, h) in enumerate(((xv, h1_h), (av, a1_h), (tv, a1t_h)))]
    for d in outs:
        d.start()
    loop(n + nd + 1 + lead, total + lead, lambda t: tick(t))
    for d in outs:
        d.wait()


def forward(x, wg, wu, wd, tm, early):
    T, D = x.shape
    F = wg.shape[2]
    rows, drows = wg.shape[1], wd.shape[1]
    n, nd = F // C, D // C
    S = jax.ShapeDtypeStruct
    out = (S((n, D, W), bf16), S((n, D, W), bf16), S((nd, F, C), bf16), S((nd, F, C), bf16), S((D, T), bf16), S((T, D), bf16),
           S((T, D), bf16), S((D, T), bf16), S((n, T, C), bf16), S((n, T, W), f32))
    return pl.pallas_call(
        functools.partial(forward_kernel, tm, early),
        out_shape=out,
        in_specs=[pl.BlockSpec(memory_space=pl.ANY)] * 4,
        out_specs=[pl.BlockSpec(memory_space=pl.ANY)] * len(out),
        scratch_shapes=[
            pltpu.VMEM((T, D), bf16), pltpu.VMEM((T, D), bf16), pltpu.VMEM((D, T), bf16), pltpu.VMEM((T, F), bf16),
            pltpu.VMEM((2, T, W), f32), pltpu.VMEM((2, D, W), bf16), pltpu.VMEM((2, F, C), bf16),
            pltpu.VMEM((rows, 2 * F), bf16), pltpu.VMEM((rows, 2 * F), bf16), pltpu.VMEM((2, drows, D), bf16),
            dma((3,)), dma((4,)), dma((2,)), dma(()), dma((4,)),
        ] + [dma((n,))] * 6 + [dma((nd,))] * 12 + [dma((early,))] * 6,
        compiler_params=pltpu.CompilerParams(collective_id=0, has_side_effects=True, vmem_limit_bytes=62 * 2**20),
        name="forward",
    )(x, wg, wu, wd)
class Scatter:
    def __init__(self, where, sems):
        self.z, self.y, self.x, self.c, (self.p1, self.p2), (self.q1, self.q2) = where
        self.xo, self.yo = (self.x + 2) % 4, (self.y + 2) % 4
        self.o = 1 - self.c
        self.snd, self.rcv = sems

    def put(self, src, dst, i, k, x=None, y=None, c=None):
        x, y, c = (self.x if x is None else x), (self.y if y is None else y), (self.c if c is None else c)
        return pltpu.make_async_remote_copy(src, dst, self.snd.at[i, k], self.rcv.at[i, k], device_id=(self.z, y, 2 * x + c), device_id_type=MESH)

    def stage(self, i, t):
        if i > 0:
            k, r = self.whole(i - 1, t)
            pltpu.make_async_copy(r, r, self.snd.at[i - 1, k]).wait()
            pltpu.make_async_copy(r, r, self.rcv.at[i - 1, k]).wait()
            self.work(i, t)
        for d in self.sent(i, t):
            d.start()

    def tick(self, t, units, mid):
        for i in reversed(range(len(self.due))):
            lag, when = self.due[i]
            if when == mid:
                u = t - lag

                @pl.when((u >= 0) & (u < units))
                def _(i=i, u=u):
                    self.stage(i, u)


def wide(v):
    return v.astype(f32)


class ScatterUp(Scatter):
    due = ((1, 0), (1, 1), (3, 0), (4, 1), (5, 1), (6, 1), (7, 1), (8, 1))

    def __init__(self, where, sems, *refs):
        super().__init__(where, sems)
        self.keep, self.give, self.l0, self.s1, self.l1, self.s2, self.l2, self.s3, self.l3, self.kg, self.s4, self.l4, self.gf = refs
        self.rows, self.q = self.l2.shape[1], self.l4.shape[1]

    def final(self, u, j):
        return self.gf.at[u, ds(j, self.q), :]

    def sent(self, i, u):
        k, h = u % SLOTS, u % 2
        if i == 0:
            return [self.put(self.give, self.l0.at[k], i, k, c=self.o)]
        if i == 1:
            return [self.put(self.s1.at[h], self.l1.at[k], i, k, x=self.p1)]
        if i == 2:
            return [self.put(self.s2.at[h], self.l2.at[k], i, k, x=self.p2)]
        if i == 3:
            return [self.put(self.s3.at[h], self.l3.at[k], i, k, y=self.q1)]
        if i == 4:
            return [self.put(self.s4.at[h], self.l4.at[k], i, k, y=self.q2)]
        if i == 5:
            return [self.put(self.final(u, self.y), self.final(u, self.y), i, k, y=self.q2)]
        if i == 6:
            return [self.put(self.final(u, j), self.final(u, j), i, k, y=self.q1) for j in (self.y, self.q2)]
        return []

    def whole(self, i, u):
        k = u % SLOTS
        refs = (self.l0.at[k], self.l1.at[k], self.l2.at[k], self.l3.at[k], self.l4.at[k], self.gf.at[u, ds(0, self.q), :],
                self.gf.at[u, ds(0, 2 * self.q), :])
        return k, refs[i]

    def pair(self, k, b):
        return wide(self.keep[k, ds(b, self.rows), :]) + wide(self.l0[k, ds(b, self.rows), :])

    def work(self, i, u):
        k, h = u % SLOTS, u % 2
        if i == 1:
            self.s1[h, 0] = self.pair(k, self.p1).astype(bf16)
            self.s1[h, 1] = self.pair(k, self.xo).astype(bf16)
        elif i == 2:
            self.s2[h] = (self.pair(k, self.p2) + wide(self.l1[k, 1])).astype(bf16)
        elif i == 3:
            for j, (to, at) in enumerate(((self.q1, 0), (self.yo, 1), (self.y, 0), (self.q2, 1))):
                r = ds(to, self.q)
                rb = pl.ds(pl.multiple_of(self.x * self.rows + to * self.q, self.q), self.q)
                g = (wide(self.keep[k, rb, :]) + wide(self.l0[k, rb, :])) + (wide(self.l1[k, 0, r, :]) + wide(self.l2[k, r, :]))
                if j < 2:
                    self.s3[h, at] = g.astype(bf16)
                else:
                    self.kg[k, at] = g
        elif i == 4:
            self.s4[h] = (self.kg[k, 1] + wide(self.l3[k, 1])).astype(bf16)
        elif i == 5:
            self.gf[u, ds(self.y, self.q), :] = (self.kg[k, 0] + wide(self.l3[k, 0]) + wide(self.l4[k])).astype(bf16)


class ScatterDown(Scatter):
    due = ((1, 0), (1, 1), (3, 0), (4, 1))

    def __init__(self, where, sems, count, *refs):
        super().__init__(where, sems)
        self.keep, self.give, self.m0, self.t1, self.m1, self.t2, self.m2, self.part = refs
        self.count, self.q = count, self.m2.shape[2]

    def sent(self, i, u):
        k, h = u % SLOTS, u % 2
        if i == 0:
            return [self.put(self.give.at[h], self.m0.at[k], i, k, c=self.o)]
        if i == 1:
            return [self.put(self.t1.at[h], self.m1.at[k], i, k, y=self.q1)]
        if i == 2:
            return [self.put(self.t2.at[h], self.m2.at[k], i, k, y=self.q2)]
        return []

    def whole(self, i, u):
        k = u % SLOTS
        return k, (self.m0.at[k], self.m1.at[k], self.m2.at[k])[i]

    def pair(self, k, j):
        return wide(self.keep[k, :, ds(j, self.q)]) + wide(self.m0[k, :, ds(j, self.q)])

    def work(self, i, u):
        k, h = u % SLOTS, u % 2
        if i == 1:
            self.t1[h, 0] = self.pair(k, self.q1).astype(bf16)
            self.t1[h, 1] = self.pair(k, self.yo).astype(bf16)
        elif i == 2:
            self.t2[h] = (self.pair(k, self.q2) + wide(self.m1[k, 1])).astype(bf16)
        elif i == 3:
            n, late = self.m2.shape[1], u // self.count
            self.part[1 - late, ds(u - late * self.count, n), :] = (self.pair(k, self.y) + (wide(self.m1[k, 0]) + wide(self.m2[k]))).astype(bf16)


class ScatterEnd(Scatter):
    def __init__(self, where, sems, part, n1, u, n2, w, dg):
        super().__init__(where, sems)
        self.part, self.n1, self.u, self.n2, self.w, self.dg = part, n1, u, n2, w, dg
        self.rows = n2.shape[1]

    def sent(self, i, l):
        here, there = 4 * self.c + self.y, 4 * (self.o) + self.y
        dg = self.dg
        if i == 0:
            return [self.put(self.part.at[l, ds(b, self.rows), :], self.n1.at[l, j], 0, l, x=self.p1) for j, b in enumerate((self.p1, self.xo))]
        if i == 1:
            return [self.put(self.u.at[l], self.n2.at[l], 1, l, x=self.p2)]
        if i == 2:
            return [self.put(self.w.at[l], dg.at[l, here], 2, l, c=self.o)]
        if i == 3:
            return [self.put(dg.at[l, j], dg.at[l, j], 3, l, y=self.q2) for j in (here, there)]
        if i == 4:
            js = [here, there, 4 * self.c + self.q2, 4 * (self.o) + self.q2]
            return [self.put(dg.at[l, j], dg.at[l, j], 4, l, y=self.q1) for j in js]
        return []

    def whole(self, i, l):
        refs = (self.n1.at[l], self.n2.at[l], self.w.at[l], self.dg.at[l, pl.ds(0, 2)], self.dg.at[l, pl.ds(0, 4)])
        return l, refs[i]

    def work(self, i, l):
        h = self.rows // 2
        if i == 1:
            self.u[l] = (wide(self.part[l, ds(self.p2, self.rows), :]) + wide(self.n1[l, 1])).astype(bf16)
        elif i == 2:
            for mine, c in ((True, self.c), (False, self.o)):
                r = ds(c, h)
                rp = pl.ds(pl.multiple_of(self.x * self.rows + c * h, h), h)
                v = (wide(self.part[l, rp, :]) + (wide(self.n1[l, 0, r, :]) + wide(self.n2[l, r, :]))).astype(bf16)
                if mine:
                    self.dg[l, 4 * self.c + self.y] = v
                else:
                    self.w[l] = v


SLOTS = 5
AHEAD = 8


def backward_kernel(tm, early, dy_h, _, fd0, fd1, a0t_h, h1_h, a1_h, a1t_h, act_h, ab_h, fgu1, gf_h, dg_h,
                    av, atv, dyv, dytv, acc, wv, wdv, actv, dguv,
                    keep, give, l0, s1, l1, s2, l2, s3, l3, kg, s4, l4, gf, dkeep, dgive, m0, t1, m1, t2, m2, part, n1, eu, n2, ew, dg,
                    isem, wsem, us, ur, dsd, dr, es, er, *gs):
    T, D = dy_h.shape
    n = fgu1.shape[0]
    nd = D // C
    nn = n + n
    half = D // 2
    rows = l2.shape[1]
    where = place()
    z, y, x, c, xs, ys = where
    ins = [pltpu.make_async_copy(a, b, isem.at[i]) for i, (a, b) in enumerate(((a1_h, av), (a1t_h, atv), (dy_h, dyv)))]
    for d in ins:
        d.start()

    def load_up(k, slot):
        return pltpu.make_async_copy(fgu1.at[k], wv.at[slot], wsem.at[0, slot])

    def start_down(fd, k, slot):
        for j in range(nd):
            pltpu.make_async_copy(fd.at[j, ds(k, C), :], wdv.at[slot, :, ds(j, C)], wsem.at[1, slot]).start()

    def wait_down(slot):
        pltpu.make_async_copy(wdv.at[slot], wdv.at[slot], wsem.at[1, slot]).wait()

    load_up(0, 0).start()
    start_down(fd1, 0, 0)
    barrier(z, y, x, c, xs)
    g1 = Gather(where, None, fgu1, rows, W, gs)
    up = ScatterUp(where, (us, ur), keep, give, l0, s1, l1, s2, l2, s3, l3, kg, s4, l4, gf)
    down = ScatterDown(where, (dsd, dr), n, dkeep, dgive, m0, t1, m1, t2, m2, part)
    end = ScatterEnd(where, (es, er), part, n1, eu, n2, ew, dg)

    def gather_tick(t):
        for i in range(5):
            @pl.when((t >= i) & (t < n - early + i))
            def _(i=i):
                g1.stage(i, t - i + early)

    def end_tick(t, l):
        for i in range(6):
            @pl.when(t == 2 * i)
            def _(i=i):
                end.stage(i, l)

    def turn_dy(r, v):
        turned(dytv, r, v, half, c)

    for d in ins:
        d.wait()

    def turn(i):
        r = ds(i, R)
        turn_dy(r, dyv[r, :])
    loop(0, T // R, turn)
    acc[...] = jnp.zeros_like(acc)

    def up_gradient(u):
        g = dot(atv[...], dguv[...], NN).astype(bf16)
        keep[u % SLOTS] = g[:half]
        give[...] = g[half:]

    def down_gradient(act, u):
        g = dot(dytv[...], act, NN).astype(bf16).T
        dkeep[u % SLOTS] = g[:, :half]
        dgive[u % 2] = g[:, half:]

    def layer1(k):
        slot = k % 2
        up.tick(k, nn, 0)
        down.tick(k, nn, 0)
        gather_tick(k)

        @pl.when(k + 1 < n)
        def _():
            load_up(k + 1, 1 - slot).start()
            start_down(fd1, k + 1, 1 - slot)
        load_up(k, slot).wait()
        wait_down(slot)
        for i in range(T // tm):
            r = pl.ds(i * tm, tm)
            gu = dot(av[r, :], wv[slot], NN)
            d = wide(dot(dyv[r, :], wdv[slot], NT).astype(bf16))
            g, u = gu[:, :C], gu[:, C:]
            sg = 0.5 + 0.5 * jnp.tanh(0.5 * g)
            b = g * sg
            actv[0, r, :] = (b * u).astype(bf16)
            dguv[r, :C] = (d * (u * (sg + b * (1 - sg)))).astype(bf16)
            dguv[r, C:] = (d * b).astype(bf16)
        up.tick(k, nn, 1)
        down.tick(k, nn, 1)
        down_gradient(actv[0], k)
        up_gradient(k)
        for j in range(2):
            acc[j] += dot(dguv[...], wv[slot, ds(j, half), :], NT)
    loop(0, n, layer1)

    def load_act(k, slot):
        return pltpu.make_async_copy(act_h.at[k], actv.at[slot], wsem.at[2, slot])

    load_act(0, 0).start()
    h_in = pltpu.make_async_copy(h1_h, av, isem.at[0])
    h_in.start()
    at_in = pltpu.make_async_copy(a0t_h, atv, isem.at[1])
    at_in.start()
    start_down(fd0, 0, 0)
    h_in.wait()

    def between(i):
        r = ds(i, R)
        h = wide(av[r, :])
        scale = lax.rsqrt(jnp.mean(h * h, -1, keepdims=True) + 1e-6)
        da = wide(jnp.concatenate([acc[0, r, :], acc[1, r, :]], axis=1).astype(bf16))
        dh = scale * (da - h * (scale * scale) * jnp.mean(da * h, -1, keepdims=True))
        v = (wide(dyv[r, :]) + wide(dh.astype(bf16))).astype(bf16)
        dyv[r, :] = v
        turn_dy(r, v)
    loop(0, T // R, between)

    def load_ab(k, slot):
        return pltpu.make_async_copy(ab_h.at[k], acc.at[slot], wsem.at[3, slot])

    load_ab(0, 0).start()

    def layer0_down(k):
        slot = k % 2
        down.tick(n + k, nn, 0)

        @pl.when(k + 1 < n)
        def _():
            load_act(k + 1, 1 - slot).start()
        load_act(k, slot).wait()

    def ahead(k):
        layer0_down(k)
        end_tick(k - 4, 1)
        down_gradient(actv[k % 2], n + k)
        down.tick(n + k, nn, 1)
    loop(0, AHEAD, ahead)
    at_in.wait()

    def layer0(k, both):
        slot = k % 2
        up.tick(n + k, nn, 0)

        @pl.when(k + 1 < n)
        def _():
            load_ab(k + 1, 1 - slot).start()
            start_down(fd0, k + 1, 1 - slot)
        if both:
            layer0_down(k + AHEAD)
        else:
            down.tick(n + AHEAD + k, nn, 0)
        end_tick(k + AHEAD - 4, 1)
        end_tick(k - (n - AHEAD + 4), 0)
        load_ab(k, slot).wait()
        wait_down(slot)
        for i in range(T // tm):
            r = pl.ds(i * tm, tm)
            d = wide(dot(dyv[r, :], wdv[slot], NT).astype(bf16))
            dguv[r, :C] = (d * acc[slot, r, :C]).astype(bf16)
            dguv[r, C:] = (d * acc[slot, r, C:]).astype(bf16)
        if both:
            down_gradient(actv[(k + AHEAD) % 2], n + AHEAD + k)
        up.tick(n + k, nn, 1)
        down.tick(n + AHEAD + k, nn, 1)
        up_gradient(n + k)
    loop(0, n - AHEAD, lambda k: layer0(k, True))
    loop(n - AHEAD, n, lambda k: layer0(k, False))

    def rest(t):
        up.tick(n + t, nn, 0)
        end_tick(t - (n - AHEAD + 4), 0)
        up.tick(n + t, nn, 1)
    loop(n, n + up.due[-1][0], rest)
    outs = [pltpu.make_async_copy(gf, gf_h, isem.at[0]), pltpu.make_async_copy(dg, dg_h, isem.at[1])]
    for d in outs:
        d.start()
    for d in outs:
        d.wait()


def backward(dy, fgu1, fd0, fd1, a0t, h1, a1, a1t, act, ab, tm, early):
    T, D = dy.shape
    n = fgu1.shape[0]
    F = n * C
    rows, drows = D // 8, F // 8
    nn = n + n
    S = jax.ShapeDtypeStruct
    out = (S(fgu1.shape, bf16), S((nn, rows, W), bf16), S((2, 8, drows, rows), bf16))
    q, w = rows // 4, W

    def V(*shape, dtype=bf16):
        return pltpu.VMEM(shape, dtype)
    return pl.pallas_call(
        functools.partial(backward_kernel, tm, early),
        out_shape=out,
        in_specs=[pl.BlockSpec(memory_space=pl.ANY)] * 10,
        out_specs=[pl.BlockSpec(memory_space=pl.ANY)] * 3,
        input_output_aliases={1: 0},
        scratch_shapes=[
            V(T, D), V(D, T), V(T, D), V(D, T), V(2, T, w, dtype=f32), V(2, D, w), V(2, C, D), V(2, T, C), V(T, w),
            V(SLOTS, D // 2, w), V(D // 2, w), V(SLOTS, D // 2, w), V(2, 2, rows, w), V(SLOTS, 2, rows, w), V(2, rows, w), V(SLOTS, rows, w),
            V(2, 2, q, w), V(SLOTS, 2, q, w), V(SLOTS, 2, q, w, dtype=f32), V(2, q, w), V(SLOTS, q, w), V(nn, rows, w),
            V(SLOTS, C, D // 2), V(2, C, D // 2), V(SLOTS, C, D // 2), V(2, 2, C, rows), V(SLOTS, 2, C, rows), V(2, C, rows), V(SLOTS, C, rows),
            V(2, F, rows), V(2, 2, 2 * drows, rows), V(2, 2 * drows, rows), V(2, 2 * drows, rows), V(2, drows, rows), V(2, 8, drows, rows),
            dma((3,)), dma((4, 2)), dma((7, SLOTS)), dma((7, SLOTS)), dma((3, SLOTS)), dma((3, SLOTS)), dma((5, 2)), dma((5, 2)),
        ] + [dma((n,))] * 6,
        compiler_params=pltpu.CompilerParams(collective_id=1, has_side_effects=True, vmem_limit_bytes=63 * 2**20),
        name="backward",
    )(dy, fgu1, fd0, fd1, a0t, h1, a1, a1t, act, ab)


def adamw(w, m, v, g):
    m = 0.9 * m + 0.1 * g
    v = 0.95 * v + 0.05 * g * g
    step = m * lax.rsqrt(v + 1e-8) + 0.1 * w
    return (w - 0.02 * step).astype(bf16), m, v


def update_kernel(gf, dg, wg, wu, wd, mg, mu, md, vg, vu, vd, *outs):
    def one(part, at, w, m, v, g):
        for o, val in zip(outs[part::3], adamw(wide(w[at]), m[at], v[at], wide(g)), strict=True):
            o[at] = val

    n, _, w = gf.shape
    for k in range(n):
        at = (0, slice(None), pl.ds(k * C, C))
        one(0, at, wg, mg, vg, gf[k, :, :C])
        one(1, at, wu, mu, vu, gf[k, :, C:])
    w = dg.shape[3]
    for j in range(dg.shape[1]):
        one(2, (0, slice(None), pl.ds(j * w, w)), wd, md, vd, dg[0, j])


def update(gf, dg, *arrays):
    wg, wd = arrays[0], arrays[2]
    n = wg.shape[2] // C
    S = jax.ShapeDtypeStruct
    up = pl.BlockSpec((1, wg.shape[1] // PARTS, wg.shape[2]), lambda l, k: (l, k, 0))
    down = pl.BlockSpec((1, wd.shape[1] // PARTS, wd.shape[2]), lambda l, k: (l, k, 0))
    specs = [up, up, down] * 3
    gspec = [pl.BlockSpec((n, gf.shape[1] // PARTS, gf.shape[2]), lambda l, k: (1 - l, k, 0)),
             pl.BlockSpec((1, dg.shape[1], dg.shape[2] // PARTS, dg.shape[3]), lambda l, k: (l, 0, k, 0))]
    return pl.pallas_call(
        update_kernel,
        grid=(2, PARTS),
        out_shape=tuple(S(a.shape, a.dtype) for a in arrays),
        in_specs=gspec + specs,
        out_specs=specs,
        name="update",
    )(gf, dg, *arrays)


PARTS = 4
TM, EARLY = 512, 5


def solution(mesh):
    assert mesh.shape["r"] == 4 and mesh.shape["s"] == 8

    def step(x, dy, *arrays):
        _, fgu1, fd0, fd1, a0t, h1, a1, a1t, act, ab = forward(x[0], *arrays[:3], TM, EARLY)
        _, gf, dg = backward(dy[0], fgu1, fd0, fd1, a0t, h1, a1, a1t, act, ab, TM, EARLY)
        return update(gf, dg, *arrays)

    states, cut = P(("rep", "r", "s"), None, None), P(None, "s", None)
    return jax.shard_map(
        step,
        mesh=mesh,
        in_specs=(states, states) + (cut,) * 9,
        out_specs=(P("rep", "s", None),) * 9,
        check_vma=False,
    )
```

time: 783 us -> 398 us (0.51)
  Pallas kernels: 0 us -> 397 us
  matrix products: 378 us -> 0 us
  waiting for transfers between devices: 331 us -> 0 us
  local copies, waits for them, and re-layouts: 26.1 us -> 0 us
  other arithmetic: 24.8 us -> 0 us
  between operations: 14.6 us -> 0.84 us
    pallas_call x0 -> x3, Pallas kernels: none -> 397 us  [the longest x1 275 us: backward(): pl.pallas_call(functools.partial(backward_kernel, tm, early), out_shape=o...]
    dot_general x15 -> x0, matrix products: 378 us -> none  [the longest x5 137 us: layer(): gate = jnp.dot(a, w['w_gate'], preferred_element_type=jnp.float32)]
    all_gather x6 -> x0, waiting for transfers between devices: 113 us -> none  [fetched(): lax.all_gather(w[number], 's', axis=0, tiled=True)]
    reduce_scatter x6 -> x0, waiting for transfers between devices: 111 us -> none  [summed(): lax.psum_scatter(term, 's', scatter_dimension=0, tiled=True)]
    psum x1 -> x0, waiting for transfers between devices: 105 us -> none  [summed(): lax.psum(lax.psum_scatter(term, 's', scatter_dimension=0, tiled=True), 'r')]
    unnamed x42 -> x0, local copies, waits for them, and re-layouts: 19.3 us -> none
    convert_element_type x2 -> x0, other arithmetic: 16.8 us -> none  [adamw(): return ((w - 0.02 * step).astype(jnp.bfloat16), m, v)]
  transfers between devices with their start and end apart: 13 -> 0, of which waited for: 10 -> 0; matrix products, arithmetic and copies ran while one was open for 38% -> 0% of each run, Pallas kernels for 0% -> 0%
where the time goes in v1:
time: 398 us
  Pallas kernels  397 us (100%)
    pallas_call x1, Pallas kernels, backward(): pl.pallas_call(functools.partial(backward_kernel, tm, early), out_shape=o...  275 us
    pallas_call x1, Pallas kernels, forward(): pl.pallas_call(functools.partial(forward_kernel, tm, early), out_shape=ou...  102 us
    pallas_call x1, Pallas kernels, update(): pl.pallas_call(update_kernel, grid=(2, PARTS), out_shape=tuple((S(a.shape...  20.6 us

profile of v1, /device:TPU:97, one launch (start us, length us, event | category | flops | bytes accessed | tf_op | source)
XLA Modules:
  0.0 398.1 jit_solution(2384901111878488679)
XLA Ops:
  0.6 101.8 %forward.1 = (bf16[13,1024,512]{2,1,0:T(8,128)(2,1)}, bf16[13,1024,512]{2,1,0:T(8,128)(2,1)}, bf16[4,3328,256]{2,1,0:T(8,128)(2,1)}, bf16[4,3328,256]{2,1,0:T(8,...) custom-call(bf16[2048,1024]{1,0:T(8,128)(2,1)} %bitcast.3, ...), custom_call_target="tpu_custom_call" | custom-call | tf_op jit(solution)/shard_map/forward/pallas_call | solution.py:302
  102.4 274.9 %backward.1 = (bf16[13,1024,512]{2,1,0:T(8,128)(2,1)}, bf16[26,128,512]{2,1,0:T(8,128)(2,1)}, bf16[2,8,416,128]{3,2,1,0:T(8,128)(2,1)}) custom-call(bf16[2048,1024]{1,0:T(8,128)(2,1)} %bitcast.2, bf16[13,1024,512]{2,1,0:T(8,128)(2,1)} %get-tuple-element.20._, bf16[4,3328,256]{2,1,0:T(8,128)(2,1)} %get-tuple-element.21.fd0, ...), custom_call_target="tpu_custom_call", output_to_operand_aliasing={{0}: (1, {})} | custom-call | tf_op jit(solution)/shard_map/backward/pallas_call | solution.py:688
  377.3 20.6 %update.1 = (bf16[2,128,3328]{2,1,0:T(8,128)(2,1)}, bf16[2,128,3328]{2,1,0:T(8,128)(2,1)}, bf16[2,416,1024]{2,1,0:T(8,128)(2,1)}, f32[2,128,3328]{2,1,0:T(8,128)...) custom-call(bf16[26,128,512]{2,1,0:T(8,128)(2,1)} %get-tuple-element, ...), custom_call_target="tpu_custom_call" | custom-call | tf_op jit(solution)/shard_map/update/pallas_call | solution.py:738

commit v2 on v1

--- a/solution.py
+++ b/solution.py
@@ -22,7 +22,7 @@
     return pl.ds(pl.multiple_of(i * n, n), n)
 
 
-def loop(first, last, f):
+def loop(last, f, first=0):
     def body(i, _):
         f(i)
         return 0
@@ -46,6 +46,7 @@
     for o in others:
         pl.semaphore_signal(sem, inc=1, device_id=o, device_id_type=MESH)
     pl.semaphore_wait(sem, len(others))
+    return others
 
 
 class Gather:
@@ -155,7 +156,7 @@
     def one(k):
         for j, w in ((0, w_g), (1, w_u)):
             pltpu.make_async_copy(w.at[l, :, ds(k, C)], own.at[:, ds(2 * k + j, C)], sem).start()
-    loop(0, own.shape[1] // (W), one)
+    loop(own.shape[1] // (W), one)
 
 
 def forward_kernel(tm, early, x_h, wg_h, wu_h, wd_h, fgu0, fgu1, fd0, fd1, a0t_h, h1_h, a1_h, a1t_h, act_h, ab_h,
@@ -190,12 +191,19 @@
     units = ((g0, 0, n), (d0, n, nd), (d1, n + nd, nd), (g1, n + 2 * nd, early))
     total = n + 2 * nd + early
 
-    def tick(t):
+    def tick(t, lo=None, hi=None):
+        lo, hi = (t, t) if lo is None else (lo, hi)
         for i, lag in enumerate(LAGS):
-            u = t - lag
             for g, base, count in units:
-                @pl.when((u >= base) & (u < base + count))
-                def _(g=g, i=i, k=u - base):
+                first, last = base + lag, base + lag + count - 1
+                if hi < first or lo > last:
+                    continue
+                if lo >= first and hi <= last:
+                    g.stage(i, t - first)
+                    continue
+
+                @pl.when((t >= first) & (t <= last))
+                def _(g=g, i=i, k=t - first):
                     g.stage(i, k)
 
     lead = LAGS[-1]
@@ -203,7 +211,7 @@
         tick(t)
     din.wait()
     for i, (own, full) in enumerate(kept):
-        loop(0, full.shape[0], lambda k, i=i: keep(i, k).start())
+        loop(full.shape[0], lambda k, i=i: keep(i, k).start())
     xin.wait()
 
     def start(i):
@@ -211,10 +219,10 @@
         a = norm(xv[r, :])
         av[r, :] = a
         turned(tv, r, a, rows, c)
-    loop(0, T // R, start)
+    loop(T // R, start)
     out0 = pltpu.make_async_copy(tv, a0t_h, isem.at[0])
     out0.start()
-    loop(2, lead, lambda t: tick(t))
+    loop(lead, lambda t: tick(t, 2, lead - 1), 2)
     for i, (own, full) in enumerate(kept):
         pltpu.make_async_copy(own, own, own_sem.at[i]).wait()
 
@@ -229,7 +237,7 @@
 
     def up(k):
         slot = k % 2
-        tick(k + 1 + lead)
+        tick(k + 1 + lead, 1 + lead, n + lead)
 
         @pl.when(k + 1 < n)
         def _():
@@ -251,7 +259,7 @@
             abv[slot, r, C:] = b
         abstore(k, slot).start()
         pltpu.make_async_copy(actv.at[:, ds(k, C)], act_h.at[k], actsem).start()
-    loop(0, n, up)
+    loop(n, up)
 
     def dload(j, slot):
         return pltpu.make_async_copy(fd0.at[j], wdv.at[slot], wsem.at[2 + slot])
@@ -261,7 +269,7 @@
 
     def down(j):
         slot = j % 2
-        tick(n + j + 1 + lead)
+        tick(n + j + 1 + lead, n + 1 + lead, n + nd + lead)
 
         @pl.when(j + 1 < nd)
         def _():
@@ -270,7 +278,7 @@
         for i in range(T // tm):
             r = pl.ds(i * tm, tm)
             av[r, ds(j, C)] = dot(actv[r, :], wdv[slot], NN).astype(bf16)
-    loop(0, nd, down)
+    loop(nd, down)
     for k in (n - 2, n - 1):
         abstore(k, k % 2).wait()
     pltpu.make_async_copy(act_h, act_h, actsem).wait()
@@ -282,11 +290,11 @@
         a = norm(h)
         av[r, :] = a
         turned(tv, r, a, rows, c)
-    loop(0, T // R, mid)
+    loop(T // R, mid)
     outs = [pltpu.make_async_copy(v, h, isem.at[i]) for i, (v, h) in enumerate(((xv, h1_h), (av, a1_h), (tv, a1t_h)))]
     for d in outs:
         d.start()
-    loop(n + nd + 1 + lead, total + lead, lambda t: tick(t))
+    loop(total + lead, lambda t: tick(t, n + nd + 1 + lead, total + lead - 1), n + nd + 1 + lead)
     for d in outs:
         d.wait()
 
@@ -487,7 +495,7 @@
 
 
 SLOTS = 5
-AHEAD = 8
+AHEAD = 7
 
 
 def backward_kernel(tm, early, dy_h, _, fd0, fd1, a0t_h, h1_h, a1_h, a1t_h, act_h, ab_h, fgu1, gf_h, dg_h,
@@ -502,7 +510,7 @@
     rows = l2.shape[1]
     where = place()
     z, y, x, c, xs, ys = where
-    ins = [pltpu.make_async_copy(a, b, isem.at[i]) for i, (a, b) in enumerate(((a1_h, av), (a1t_h, atv), (dy_h, dyv)))]
+    ins = [pltpu.make_async_copy(a, b, isem.at[i]) for i, (a, b) in enumerate(((dy_h, dyv), (a1_h, av), (a1t_h, atv)))]
     for d in ins:
         d.start()
 
@@ -539,14 +547,15 @@
     def turn_dy(r, v):
         turned(dytv, r, v, half, c)
 
-    for d in ins:
-        d.wait()
+    acc[...] = jnp.zeros_like(acc)
+    ins[0].wait()
 
     def turn(i):
         r = ds(i, R)
         turn_dy(r, dyv[r, :])
-    loop(0, T // R, turn)
-    acc[...] = jnp.zeros_like(acc)
+    loop(T // R, turn)
+    for d in ins[1:]:
+        d.wait()
 
     def up_gradient(u):
         g = dot(atv[...], dguv[...], NN).astype(bf16)
@@ -586,7 +595,7 @@
         up_gradient(k)
         for j in range(2):
             acc[j] += dot(dguv[...], wv[slot, ds(j, half), :], NT)
-    loop(0, n, layer1)
+    loop(n, layer1)
 
     def load_act(k, slot):
         return pltpu.make_async_copy(act_h.at[k], actv.at[slot], wsem.at[2, slot])
@@ -608,7 +617,7 @@
         v = (wide(dyv[r, :]) + wide(dh.astype(bf16))).astype(bf16)
         dyv[r, :] = v
         turn_dy(r, v)
-    loop(0, T // R, between)
+    loop(T // R, between)
 
     def load_ab(k, slot):
         return pltpu.make_async_copy(ab_h.at[k], acc.at[slot], wsem.at[3, slot])
@@ -629,7 +638,7 @@
         end_tick(k - 4, 1)
         down_gradient(actv[k % 2], n + k)
         down.tick(n + k, nn, 1)
-    loop(0, AHEAD, ahead)
+    loop(AHEAD, ahead)
     at_in.wait()
 
     def layer0(k, both):
@@ -658,14 +667,14 @@
         up.tick(n + k, nn, 1)
         down.tick(n + AHEAD + k, nn, 1)
         up_gradient(n + k)
-    loop(0, n - AHEAD, lambda k: layer0(k, True))
-    loop(n - AHEAD, n, lambda k: layer0(k, False))
+    loop(n - AHEAD, lambda k: layer0(k, True))
+    loop(n, lambda k: layer0(k, False), n - AHEAD)
 
     def rest(t):
         up.tick(n + t, nn, 0)
         end_tick(t - (n - AHEAD + 4), 0)
         up.tick(n + t, nn, 1)
-    loop(n, n + up.due[-1][0], rest)
+    loop(n + up.due[-1][0], rest, n)
     outs = [pltpu.make_async_copy(gf, gf_h, isem.at[0]), pltpu.make_async_copy(dg, dg_h, isem.at[1])]
     for d in outs:
         d.start()

time: 398 us -> 393 us (0.987)
  Pallas kernels: 397 us -> 392 us
    pallas_call x1, Pallas kernels: 275 us -> 270 us  [backward(): pl.pallas_call(functools.partial(backward_kernel, tm, early), out_shape=o...]
where the time goes in v2:
time: 393 us; the launch traced here: 392 us
  Pallas kernels  392 us (100%)
    pallas_call x1, Pallas kernels, backward(): pl.pallas_call(functools.partial(backward_kernel, tm, early), out_shape=o...  270 us
    pallas_call x1, Pallas kernels, forward(): pl.pallas_call(functools.partial(forward_kernel, tm, early), out_shape=ou...  101 us
    pallas_call x1, Pallas kernels, update(): pl.pallas_call(update_kernel, grid=(2, PARTS), out_shape=tuple((S(a.shape...  20.6 us

profile of v2, /device:TPU:97, one launch (start us, length us, event | category | flops | bytes accessed | tf_op | source)
XLA Modules:
  0.0 392.4 jit_solution(13785437707360452723)
XLA Ops:
  0.6 101.2 %forward.1 = (bf16[13,1024,512]{2,1,0:T(8,128)(2,1)}, bf16[13,1024,512]{2,1,0:T(8,128)(2,1)}, bf16[4,3328,256]{2,1,0:T(8,128)(2,1)}, bf16[4,3328,256]{2,1,0:T(8,...) custom-call(bf16[2048,1024]{1,0:T(8,128)(2,1)} %bitcast.3, ...), custom_call_target="tpu_custom_call" | custom-call | tf_op jit(solution)/shard_map/forward/pallas_call | solution.py:310
  101.8 269.8 %backward.1 = (bf16[13,1024,512]{2,1,0:T(8,128)(2,1)}, bf16[26,128,512]{2,1,0:T(8,128)(2,1)}, bf16[2,8,416,128]{3,2,1,0:T(8,128)(2,1)}) custom-call(bf16[2048,1024]{1,0:T(8,128)(2,1)} %bitcast.2, bf16[13,1024,512]{2,1,0:T(8,128)(2,1)} %get-tuple-element.20._, bf16[4,3328,256]{2,1,0:T(8,128)(2,1)} %get-tuple-element.21.fd0, ...), custom_call_target="tpu_custom_call", output_to_operand_aliasing={{0}: (1, {})} | custom-call | tf_op jit(solution)/shard_map/backward/pallas_call | solution.py:697
  371.7 20.6 %update.1 = (bf16[2,128,3328]{2,1,0:T(8,128)(2,1)}, bf16[2,128,3328]{2,1,0:T(8,128)(2,1)}, bf16[2,416,1024]{2,1,0:T(8,128)(2,1)}, f32[2,128,3328]{2,1,0:T(8,128)...) custom-call(bf16[26,128,512]{2,1,0:T(8,128)(2,1)} %get-tuple-element, ...), custom_call_target="tpu_custom_call" | custom-call | tf_op jit(solution)/shard_map/update/pallas_call | solution.py:747
